TPU v7x, 8 devices: a whole 2x2x1 slice. The times are simulated.
8 devices in a mesh: pairs: 2 (over z, y), rows: 4 (over x, core).
Axes of the slice: x: 2, y: 2, z: 1, core: 2. Of those that a mesh axis runs over, the one named last changes fastest.
Arguments:
- cost_src: float32 [4096, 2048], P(('pairs', 'rows')), parts along dimension 0
- cost_tgt: float32 [2048, 1024], P(('pairs', 'rows')), parts along dimension 0
- plan_init: float32 [4096, 1024], P(('pairs', 'rows')), parts along dimension 0
- mass_src: float32 [4096], P(('pairs', 'rows')), parts along dimension 0
- mass_tgt: float32 [2048], P('pairs'), parts along dimension 0
- feat_src: float32 [4096, 256], P(('pairs', 'rows')), parts along dimension 0
- feat_tgt: float32 [2048, 256], P(('pairs', 'rows')), parts along dimension 0
- epsilon: float32 [], replicated
Outputs:
- output: float32 [4096, 1024], P(('pairs', 'rows')), parts along dimension 0
There are 2 independent parts. A program takes and returns all parts, laid end to end along the dimension named above; an argument that names none is the same for every part.
All inputs are finite; a program needn't handle non-finite values.
Results may differ from a plain program's by a relative error of at most 0.001.
Values are sent between devices in bfloat16 or wider.
A program may use at most 1 GiB of HBM per device.

v0:
```python
import jax
import jax.numpy as jnp
from jax import lax
from jax.sharding import PartitionSpec as P

ALPHA = 0.5
OUTER_STEPS = 2
SWEEPS = 10


def gibbs_kernel(cost_rows, epsilon):
    return jnp.exp(-(cost_rows - jnp.min(cost_rows, axis=1, keepdims=True)) / epsilon)


def scaled_plan(kernel, mass_rows, mass_tgt):
    def value_a14(sweep_index, scales):
        row_scale = mass_rows / jnp.sum(kernel * scales[1][None, :], axis=1)
        col_sum = lax.psum(jnp.sum(kernel * row_scale[:, None], axis=0), 'rows')
        return row_scale, mass_tgt / col_sum
    start_scales = (jnp.ones_like(mass_rows), jnp.ones_like(mass_tgt))
    row_scale, col_scale = lax.fori_loop(0, SWEEPS, value_a14, start_scales)
    return row_scale[:, None] * kernel * col_scale[None, :]


def solution(mesh):
    def local_fgw(cost_src, cost_tgt, plan_init, mass_src, mass_tgt, feat_src, feat_tgt, epsilon):
        src_half = cost_src.astype(jnp.bfloat16)
        tgt_half = cost_tgt.astype(jnp.bfloat16)
        feat_all = lax.all_gather(feat_tgt.astype(jnp.bfloat16), 'rows', tiled=True)
        cross_term = jnp.einsum('id,jd->ij', feat_src.astype(jnp.bfloat16), feat_all, preferred_element_type=jnp.float32)
        feat_cost = (-2.0 * ALPHA) * cross_term
        transport = plan_init
        for step_index in range(OUTER_STEPS):
            transport_all = lax.all_gather(transport.astype(jnp.bfloat16), 'rows', tiled=True)
            tgt_all = lax.all_gather(tgt_half, 'rows', tiled=True)
            prod_a = jnp.dot(src_half, transport_all, preferred_element_type=jnp.float32)
            prod_b = jnp.dot(prod_a.astype(jnp.bfloat16), tgt_all, preferred_element_type=jnp.float32)
            step_cost = feat_cost - (2.0 * (1.0 - ALPHA)) * prod_b
            transport = scaled_plan(gibbs_kernel(step_cost, epsilon), mass_src, mass_tgt)
        return transport

    row_spec = P(('pairs', 'rows'), None)
    vec_spec = P(('pairs', 'rows'))
    in_specs = (row_spec, row_spec, row_spec, vec_spec, P('pairs'), row_spec, row_spec, P())
    return jax.shard_map(local_fgw, mesh=mesh, in_specs=in_specs, out_specs=row_spec, check_vma=False)
```

profile of v0, /device:TPU:0, one launch (start us, length us, event | category | flops | bytes accessed | tf_op | source)
XLA Modules:
  0.0 266.2 jit_solution(7473629115343291775)
XLA Ops:
  6.5 2.3 convert_element_type.30
  8.9 1.1 convert_element_type.28
  10.8 16.2 %all_gather.13 = bf16[1024,256]{1,0:T(8,128)(2,1)S(1)} all-gather(bf16[256,256]{1,0:T(8,128)(2,1)S(1)} %convert_element_type.26), channel_id=1, replica_groups=mesh['pairs'=2,'rows'=4] {'rows'}, dimensions={0}, use_global_device_ids=true | all-gather | bytes 655360 | tf_op jit(solution)/shard_map/all_gather | solution.py:29
  27.1 0.5 fusion.6
  27.6 6.6 %all-gather.6.cloned.1.call-done = bf16[1024,1024]{1,0:T(8,128)(2,1)} async-done(((bf16[256,1024]{1,0:T(8,128)(2,1)}), bf16[1024,1024]{1,0:T(8,128)(2,1)}) %all-gather.6.cloned.1.call-update) | async-done | bytes 2097168 | tf_op jit(solution)/shard_map/all_gather | solution.py:35
  34.2 33.6 %all-gather.4.cloned.1.call-done = bf16[2048,1024]{1,0:T(8,128)(2,1)} async-done(((bf16[512,1024]{1,0:T(8,128)(2,1)}), bf16[2048,1024]{1,0:T(8,128)(2,1)}) %all-gather.4.cloned.1.call-update) | async-done | bytes 4194320 | tf_op jit(solution)/shard_map/all_gather | solution.py:34
  67.8 8.8 %fusion.8 = (f32[512]{0:T(512)S(1)}, f32[512,1024]{1,0:T(8,128)}) fusion(bf16[1024,1024]{1,0:T(8,128)(2,1)} %all-gather.6.cloned.1.call-done, bf16[2048,1024]{1,0:T(8,128)(2,1)} %all-gather.4.cloned.1.call-done, f32[512,2048]{1,0:T(8,128)} %param.12, f32[512,1024]{1,0:T(8,128)S(1)} %fusion.6), kind=kOutput, calls=%fused_computation.18 | convolution fusion | flops 3224370688 | bytes 14682112 | tf_op jit(solution)/shard_map/dot_general | solution.py:37
  76.6 2.0 divide_exponential_fusion.1
  78.6 0.6 broadcast.14.clone
  79.2 65.1 %while.26 = (s32[]{:T(128)}, f32[512]{0:T(512)}, f32[1024]{0:T(1024)S(1)}, f32[512,1024]{1,0:T(8,128)S(1)}, f32[512]{0:T(512)S(1)}, /*index=5*/f32[1024]{0:T(1024)S(1)}, s32[]{:T(128)}, s32[]{:T(128)}) while((s32[]{:T(128)}, f32[512]{0:T(512)}, f32[1024]{0:T(1024)S(1)}, f32[512,1024]{1,0:T(8,128)S(1)}, f32[512]{0:T(512)S(1)}, ...), condition=%wide.region_5.0_spmd.clone, body=%wide.region_1.0_spmd.clone.sunk | while | flops 2099203 | bytes 4249723 | solution.py:21
  79.7 5.9 %psum.18 = f32[1024]{0:T(1024)S(1)} all-reduce(f32[1024]{0:T(1024)S(1)} %multiply_reduce_fusion.9), channel_id=1, replica_groups=mesh['pairs'=2,'rows'=4] {'rows'}, use_global_device_ids=true, to_apply=%region_4.0 | all-reduce | flops 1024 | bytes 8192 | tf_op jit(solution)/shard_map/while/body/eval_jaxpr/psum | solution.py:18
  85.6 0.2 multiply_reduce_fusion.8
  86.1 5.7 %psum.18 = f32[1024]{0:T(1024)S(1)} all-reduce(f32[1024]{0:T(1024)S(1)} %multiply_reduce_fusion.9), channel_id=1, replica_groups=mesh['pairs'=2,'rows'=4] {'rows'}, use_global_device_ids=true, to_apply=%region_4.0 | all-reduce | flops 1024 | bytes 8192 | tf_op jit(solution)/shard_map/while/body/eval_jaxpr/psum | solution.py:18
  91.8 0.2 multiply_reduce_fusion.8
  92.2 6.8 %psum.18 = f32[1024]{0:T(1024)S(1)} all-reduce(f32[1024]{0:T(1024)S(1)} %multiply_reduce_fusion.9), channel_id=1, replica_groups=mesh['pairs'=2,'rows'=4] {'rows'}, use_global_device_ids=true, to_apply=%region_4.0 | all-reduce | flops 1024 | bytes 8192 | tf_op jit(solution)/shard_map/while/body/eval_jaxpr/psum | solution.py:18
  99.0 0.2 multiply_reduce_fusion.8
  99.5 5.8 %psum.18 = f32[1024]{0:T(1024)S(1)} all-reduce(f32[1024]{0:T(1024)S(1)} %multiply_reduce_fusion.9), channel_id=1, replica_groups=mesh['pairs'=2,'rows'=4] {'rows'}, use_global_device_ids=true, to_apply=%region_4.0 | all-reduce | flops 1024 | bytes 8192 | tf_op jit(solution)/shard_map/while/body/eval_jaxpr/psum | solution.py:18
  105.3 0.2 multiply_reduce_fusion.8
  105.8 6.0 %psum.18 = f32[1024]{0:T(1024)S(1)} all-reduce(f32[1024]{0:T(1024)S(1)} %multiply_reduce_fusion.9), channel_id=1, replica_groups=mesh['pairs'=2,'rows'=4] {'rows'}, use_global_device_ids=true, to_apply=%region_4.0 | all-reduce | flops 1024 | bytes 8192 | tf_op jit(solution)/shard_map/while/body/eval_jaxpr/psum | solution.py:18
  111.8 0.2 multiply_reduce_fusion.8
  112.3 5.7 %psum.18 = f32[1024]{0:T(1024)S(1)} all-reduce(f32[1024]{0:T(1024)S(1)} %multiply_reduce_fusion.9), channel_id=1, replica_groups=mesh['pairs'=2,'rows'=4] {'rows'}, use_global_device_ids=true, to_apply=%region_4.0 | all-reduce | flops 1024 | bytes 8192 | tf_op jit(solution)/shard_map/while/body/eval_jaxpr/psum | solution.py:18
  118.5 6.2 %psum.18 = f32[1024]{0:T(1024)S(1)} all-reduce(f32[1024]{0:T(1024)S(1)} %multiply_reduce_fusion.9), channel_id=1, replica_groups=mesh['pairs'=2,'rows'=4] {'rows'}, use_global_device_ids=true, to_apply=%region_4.0 | all-reduce | flops 1024 | bytes 8192 | tf_op jit(solution)/shard_map/while/body/eval_jaxpr/psum | solution.py:18
  124.7 0.2 multiply_reduce_fusion.8
  125.1 5.8 %psum.18 = f32[1024]{0:T(1024)S(1)} all-reduce(f32[1024]{0:T(1024)S(1)} %multiply_reduce_fusion.9), channel_id=1, replica_groups=mesh['pairs'=2,'rows'=4] {'rows'}, use_global_device_ids=true, to_apply=%region_4.0 | all-reduce | flops 1024 | bytes 8192 | tf_op jit(solution)/shard_map/while/body/eval_jaxpr/psum | solution.py:18
  130.9 0.2 multiply_reduce_fusion.8
  131.4 6.5 %psum.18 = f32[1024]{0:T(1024)S(1)} all-reduce(f32[1024]{0:T(1024)S(1)} %multiply_reduce_fusion.9), channel_id=1, replica_groups=mesh['pairs'=2,'rows'=4] {'rows'}, use_global_device_ids=true, to_apply=%region_4.0 | all-reduce | flops 1024 | bytes 8192 | tf_op jit(solution)/shard_map/while/body/eval_jaxpr/psum | solution.py:18
  138.0 0.2 multiply_reduce_fusion.8
  138.4 5.9 %psum.18 = f32[1024]{0:T(1024)S(1)} all-reduce(f32[1024]{0:T(1024)S(1)} %multiply_reduce_fusion.9), channel_id=1, replica_groups=mesh['pairs'=2,'rows'=4] {'rows'}, use_global_device_ids=true, to_apply=%region_4.0 | all-reduce | flops 1024 | bytes 8192 | tf_op jit(solution)/shard_map/while/body/eval_jaxpr/psum | solution.py:18
  144.3 3.4 %multiply_convert_fusion = bf16[512,1024]{1,0:T(8,128)(2,1)} fusion(f32[1024]{0:T(1024)S(1)} %get-tuple-element.70, f32[512]{0:T(512)} %get-tuple-element.69, f32[]{:T(128)S(6)} %copy.27, f32[512,1024]{1,0:T(8,128)} %get-tuple-element.138, f32[512]{0:T(512)S(1)} %get-tuple-element.137), kind=kLoop, calls=%fused_computation.8 | loop fusion | flops 3145728 | bytes 3153924 | tf_op jit(solution)/shard_map/convert_element_type | solution.py:34
  147.8 31.9 %all-gather.8.cloned.1.call-done = bf16[2048,1024]{1,0:T(8,128)(2,1)} async-done(((bf16[512,1024]{1,0:T(8,128)(2,1)}), bf16[2048,1024]{1,0:T(8,128)(2,1)}) %all-gather.8.cloned.1.call-update) | async-done | bytes 4194320 | tf_op jit(solution)/shard_map/all_gather | solution.py:34
  179.7 8.9 %fusion.11 = (f32[512]{0:T(512)S(1)}, f32[512,1024]{1,0:T(8,128)}) fusion(bf16[1024,1024]{1,0:T(8,128)(2,1)} %all-gather.6.cloned.1.call-done, bf16[2048,1024]{1,0:T(8,128)(2,1)} %all-gather.8.cloned.1.call-done, f32[512,2048]{1,0:T(8,128)} %param.12, f32[512,1024]{1,0:T(8,128)S(1)} %copy-done.2), kind=kOutput, calls=%fused_computation.19 | convolution fusion | flops 3224370688 | bytes 14682112 | tf_op jit(solution)/shard_map/dot_general | solution.py:37
  188.5 2.0 divide_exponential_fusion
  190.5 0.6 broadcast.14
  191.1 65.1 %while.27 = (s32[]{:T(128)}, f32[512]{0:T(512)}, f32[1024]{0:T(1024)S(1)}, f32[512,1024]{1,0:T(8,128)S(1)}, f32[512]{0:T(512)S(1)}, /*index=5*/f32[1024]{0:T(1024)S(1)}, s32[]{:T(128)}, s32[]{:T(128)}) while((s32[]{:T(128)}, f32[512]{0:T(512)}, f32[1024]{0:T(1024)S(1)}, f32[512,1024]{1,0:T(8,128)S(1)}, f32[512]{0:T(512)S(1)}, ...), condition=%wide.region_11.0_spmd.clone, body=%wide.region_7.0_spmd.clone.sunk | while | flops 2099203 | bytes 4249723 | solution.py:21
  191.1 0.2 multiply_reduce_fusion.10
  191.6 5.9 %psum.19 = f32[1024]{0:T(1024)S(1)} all-reduce(f32[1024]{0:T(1024)S(1)} %multiply_reduce_fusion.11), channel_id=1, replica_groups=mesh['pairs'=2,'rows'=4] {'rows'}, use_global_device_ids=true, to_apply=%region_10.0 | all-reduce | flops 1024 | bytes 8192 | tf_op jit(solution)/shard_map/while/body/eval_jaxpr/psum | solution.py:18
  197.5 0.2 multiply_reduce_fusion.10
  198.0 5.7 %psum.19 = f32[1024]{0:T(1024)S(1)} all-reduce(f32[1024]{0:T(1024)S(1)} %multiply_reduce_fusion.11), channel_id=1, replica_groups=mesh['pairs'=2,'rows'=4] {'rows'}, use_global_device_ids=true, to_apply=%region_10.0 | all-reduce | flops 1024 | bytes 8192 | tf_op jit(solution)/shard_map/while/body/eval_jaxpr/psum | solution.py:18
  203.7 0.2 multiply_reduce_fusion.10
  204.1 6.8 %psum.19 = f32[1024]{0:T(1024)S(1)} all-reduce(f32[1024]{0:T(1024)S(1)} %multiply_reduce_fusion.11), channel_id=1, replica_groups=mesh['pairs'=2,'rows'=4] {'rows'}, use_global_device_ids=true, to_apply=%region_10.0 | all-reduce | flops 1024 | bytes 8192 | tf_op jit(solution)/shard_map/while/body/eval_jaxpr/psum | solution.py:18
  211.4 5.8 %psum.19 = f32[1024]{0:T(1024)S(1)} all-reduce(f32[1024]{0:T(1024)S(1)} %multiply_reduce_fusion.11), channel_id=1, replica_groups=mesh['pairs'=2,'rows'=4] {'rows'}, use_global_device_ids=true, to_apply=%region_10.0 | all-reduce | flops 1024 | bytes 8192 | tf_op jit(solution)/shard_map/while/body/eval_jaxpr/psum | solution.py:18
  217.7 6.0 %psum.19 = f32[1024]{0:T(1024)S(1)} all-reduce(f32[1024]{0:T(1024)S(1)} %multiply_reduce_fusion.11), channel_id=1, replica_groups=mesh['pairs'=2,'rows'=4] {'rows'}, use_global_device_ids=true, to_apply=%region_10.0 | all-reduce | flops 1024 | bytes 8192 | tf_op jit(solution)/shard_map/while/body/eval_jaxpr/psum | solution.py:18
  224.2 5.7 %psum.19 = f32[1024]{0:T(1024)S(1)} all-reduce(f32[1024]{0:T(1024)S(1)} %multiply_reduce_fusion.11), channel_id=1, replica_groups=mesh['pairs'=2,'rows'=4] {'rows'}, use_global_device_ids=true, to_apply=%region_10.0 | all-reduce | flops 1024 | bytes 8192 | tf_op jit(solution)/shard_map/while/body/eval_jaxpr/psum | solution.py:18
  230.4 6.2 %psum.19 = f32[1024]{0:T(1024)S(1)} all-reduce(f32[1024]{0:T(1024)S(1)} %multiply_reduce_fusion.11), channel_id=1, replica_groups=mesh['pairs'=2,'rows'=4] {'rows'}, use_global_device_ids=true, to_apply=%region_10.0 | all-reduce | flops 1024 | bytes 8192 | tf_op jit(solution)/shard_map/while/body/eval_jaxpr/psum | solution.py:18
  237.0 5.8 %psum.19 = f32[1024]{0:T(1024)S(1)} all-reduce(f32[1024]{0:T(1024)S(1)} %multiply_reduce_fusion.11), channel_id=1, replica_groups=mesh['pairs'=2,'rows'=4] {'rows'}, use_global_device_ids=true, to_apply=%region_10.0 | all-reduce | flops 1024 | bytes 8192 | tf_op jit(solution)/shard_map/while/body/eval_jaxpr/psum | solution.py:18
  243.3 6.5 %psum.19 = f32[1024]{0:T(1024)S(1)} all-reduce(f32[1024]{0:T(1024)S(1)} %multiply_reduce_fusion.11), channel_id=1, replica_groups=mesh['pairs'=2,'rows'=4] {'rows'}, use_global_device_ids=true, to_apply=%region_10.0 | all-reduce | flops 1024 | bytes 8192 | tf_op jit(solution)/shard_map/while/body/eval_jaxpr/psum | solution.py:18
  250.3 5.9 %psum.19 = f32[1024]{0:T(1024)S(1)} all-reduce(f32[1024]{0:T(1024)S(1)} %multiply_reduce_fusion.11), channel_id=1, replica_groups=mesh['pairs'=2,'rows'=4] {'rows'}, use_global_device_ids=true, to_apply=%region_10.0 | all-reduce | flops 1024 | bytes 8192 | tf_op jit(solution)/shard_map/while/body/eval_jaxpr/psum | solution.py:18
  256.2 3.5 %multiply_multiply_fusion = f32[512,1024]{1,0:T(8,128)} fusion(f32[1024]{0:T(1024)S(1)} %get-tuple-element.72, f32[512]{0:T(512)} %get-tuple-element.71, f32[]{:T(128)S(6)} %copy.27, f32[512,1024]{1,0:T(8,128)} %get-tuple-element.140, f32[512]{0:T(512)S(1)} %get-tuple-element.139), kind=kLoop, calls=%fused_computation.6 | loop fusion | flops 2621440 | bytes 4202500 | tf_op jit(solution)/shard_map/mul | solution.py:22
  (152 shorter events, 6.8 us)
Async XLA Ops:
  6.5 2.4 copy-start
  6.5 27.7 %all-gather.6.cloned.1.call-start = ((), (), s32[]{:S(2)}) async-start(), calls=%async_computation.1 | async-start | bytes 2621440 | tf_op jit(solution)/shard_map/all_gather | solution.py:35
  8.9 1.3 copy-start.5
  8.9 18.2 %copy-start.3 = (f32[512,256]{1,0:T(8,128)S(1)}, f32[512,256]{1,0:T(8,128)}, u32[]{:S(2)}) copy-start(f32[512,256]{1,0:T(8,128)} %param.17) | copy-start | bytes 1572868
  8.9 58.9 %all-gather.4.cloned.1.call-start = ((), (), s32[]{:S(2)}) async-start(), calls=%async_computation | async-start | bytes 5242880 | tf_op jit(solution)/shard_map/all_gather | solution.py:34
  10.1 169.6 %all-gather.8.cloned.1.call-start = ((), (), s32[]{:S(2)}) async-start(), calls=%async_computation.2 | async-start | bytes 5242880 | tf_op jit(solution)/shard_map/all_gather | solution.py:34
  27.5 49.0 %copy-start.1 = (f32[512,1024]{1,0:T(8,128)}, f32[512,1024]{1,0:T(8,128)S(1)}, u32[]{:S(2)}) copy-start(f32[512,1024]{1,0:T(8,128)S(1)} %fusion.6) | copy-start | bytes 6291460
  76.6 2.6 copy-start.4
  76.6 2.6 copy-start.6
  79.5 6.1 %copy-start.8 = (f32[512]{0:T(512)}, f32[512]{0:T(512)S(1)}, u32[]{:S(2)}) copy-start(f32[512]{0:T(512)S(1)} %div.53) | copy-start | bytes 6148 | tf_op jit(solution)/shard_map/while
  85.9 5.9 %copy-start.8 = (f32[512]{0:T(512)}, f32[512]{0:T(512)S(1)}, u32[]{:S(2)}) copy-start(f32[512]{0:T(512)S(1)} %div.53) | copy-start | bytes 6148 | tf_op jit(solution)/shard_map/while
  92.0 7.0 %copy-start.8 = (f32[512]{0:T(512)}, f32[512]{0:T(512)S(1)}, u32[]{:S(2)}) copy-start(f32[512]{0:T(512)S(1)} %div.53) | copy-start | bytes 6148 | tf_op jit(solution)/shard_map/while
  99.3 6.0 %copy-start.8 = (f32[512]{0:T(512)}, f32[512]{0:T(512)S(1)}, u32[]{:S(2)}) copy-start(f32[512]{0:T(512)S(1)} %div.53) | copy-start | bytes 6148 | tf_op jit(solution)/shard_map/while
  105.5 6.3 %copy-start.8 = (f32[512]{0:T(512)}, f32[512]{0:T(512)S(1)}, u32[]{:S(2)}) copy-start(f32[512]{0:T(512)S(1)} %div.53) | copy-start | bytes 6148 | tf_op jit(solution)/shard_map/while
  112.1 5.9 %copy-start.8 = (f32[512]{0:T(512)}, f32[512]{0:T(512)S(1)}, u32[]{:S(2)}) copy-start(f32[512]{0:T(512)S(1)} %div.53) | copy-start | bytes 6148 | tf_op jit(solution)/shard_map/while
  118.2 6.4 %copy-start.8 = (f32[512]{0:T(512)}, f32[512]{0:T(512)S(1)}, u32[]{:S(2)}) copy-start(f32[512]{0:T(512)S(1)} %div.53) | copy-start | bytes 6148 | tf_op jit(solution)/shard_map/while
  124.9 6.0 %copy-start.8 = (f32[512]{0:T(512)}, f32[512]{0:T(512)S(1)}, u32[]{:S(2)}) copy-start(f32[512]{0:T(512)S(1)} %div.53) | copy-start | bytes 6148 | tf_op jit(solution)/shard_map/while
  131.2 6.8 %copy-start.8 = (f32[512]{0:T(512)}, f32[512]{0:T(512)S(1)}, u32[]{:S(2)}) copy-start(f32[512]{0:T(512)S(1)} %div.53) | copy-start | bytes 6148 | tf_op jit(solution)/shard_map/while
  138.2 6.1 %copy-start.8 = (f32[512]{0:T(512)}, f32[512]{0:T(512)S(1)}, u32[]{:S(2)}) copy-start(f32[512]{0:T(512)S(1)} %div.53) | copy-start | bytes 6148 | tf_op jit(solution)/shard_map/while
  144.3 35.3 %copy-start.2 = (f32[512,1024]{1,0:T(8,128)S(1)}, f32[512,1024]{1,0:T(8,128)}, u32[]{:S(2)}) copy-start(f32[512,1024]{1,0:T(8,128)} %copy-done.1) | copy-start | bytes 6291460
  191.4 6.1 %copy-start.7 = (f32[512]{0:T(512)}, f32[512]{0:T(512)S(1)}, u32[]{:S(2)}) copy-start(f32[512]{0:T(512)S(1)} %div.55) | copy-start | bytes 6148 | tf_op jit(solution)/shard_map/while
  197.8 5.9 %copy-start.7 = (f32[512]{0:T(512)}, f32[512]{0:T(512)S(1)}, u32[]{:S(2)}) copy-start(f32[512]{0:T(512)S(1)} %div.55) | copy-start | bytes 6148 | tf_op jit(solution)/shard_map/while
  203.9 7.0 %copy-start.7 = (f32[512]{0:T(512)}, f32[512]{0:T(512)S(1)}, u32[]{:S(2)}) copy-start(f32[512]{0:T(512)S(1)} %div.55) | copy-start | bytes 6148 | tf_op jit(solution)/shard_map/while
  211.2 6.0 %copy-start.7 = (f32[512]{0:T(512)}, f32[512]{0:T(512)S(1)}, u32[]{:S(2)}) copy-start(f32[512]{0:T(512)S(1)} %div.55) | copy-start | bytes 6148 | tf_op jit(solution)/shard_map/while
  217.4 6.3 %copy-start.7 = (f32[512]{0:T(512)}, f32[512]{0:T(512)S(1)}, u32[]{:S(2)}) copy-start(f32[512]{0:T(512)S(1)} %div.55) | copy-start | bytes 6148 | tf_op jit(solution)/shard_map/while
  224.0 5.9 %copy-start.7 = (f32[512]{0:T(512)}, f32[512]{0:T(512)S(1)}, u32[]{:S(2)}) copy-start(f32[512]{0:T(512)S(1)} %div.55) | copy-start | bytes 6148 | tf_op jit(solution)/shard_map/while
  230.1 6.4 %copy-start.7 = (f32[512]{0:T(512)}, f32[512]{0:T(512)S(1)}, u32[]{:S(2)}) copy-start(f32[512]{0:T(512)S(1)} %div.55) | copy-start | bytes 6148 | tf_op jit(solution)/shard_map/while
  236.8 6.0 %copy-start.7 = (f32[512]{0:T(512)}, f32[512]{0:T(512)S(1)}, u32[]{:S(2)}) copy-start(f32[512]{0:T(512)S(1)} %div.55) | copy-start | bytes 6148 | tf_op jit(solution)/shard_map/while
  243.1 6.8 %copy-start.7 = (f32[512]{0:T(512)}, f32[512]{0:T(512)S(1)}, u32[]{:S(2)}) copy-start(f32[512]{0:T(512)S(1)} %div.55) | copy-start | bytes 6148 | tf_op jit(solution)/shard_map/while
  250.1 6.1 %copy-start.7 = (f32[512]{0:T(512)}, f32[512]{0:T(512)S(1)}, u32[]{:S(2)}) copy-start(f32[512]{0:T(512)S(1)} %div.55) | copy-start | bytes 6148 | tf_op jit(solution)/shard_map/while
Sparse Core Ops, SparseCore 0:
  9.0 25.1 all-gather.5
  35.7 32.0 all-gather.3
  147.9 31.7 all-gather.7
where the time goes:
time: 267 us; the launch traced here: 266 us
  blocking collectives  137 us (51%)
  waiting for transfers between devices  72.2 us (27%)
  other arithmetic  23.3 us (9%)
  matrix products  18.1 us (7%)
  between operations  13.9 us (5%)
    psum x20, blocking collectives, value_a14(): col_sum = lax.psum(jnp.sum(kernel * row_scale[:, None], axis=0), 'rows')  120 us
    all_gather x2, waiting for transfers between devices, local_fgw(): lax.all_gather(transport.astype(jnp.bfloat16), 'rows', tiled=True)  65.5 us
    dot_general x2, matrix products, local_fgw(): jnp.dot(prod_a.astype(jnp.bfloat16), tgt_all, preferred_element_type=jnp....  17.7 us
    all_gather x1, blocking collectives, local_fgw(): feat_all = lax.all_gather(feat_tgt.astype(jnp.bfloat16), 'rows', tiled=True)  16.2 us
    all_gather x1, waiting for transfers between devices, local_fgw(): tgt_all = lax.all_gather(tgt_half, 'rows', tiled=True)  6.64 us
  transfers between devices with their start and end apart: 3, of which 3 were waited for; matrix products, arithmetic and copies ran while one was open for 1% of the time, Pallas kernels for 0%

commit v1 on v0

v1 whole, which is shorter than its diff:
```python
import jax
import jax.numpy as jnp
from jax import lax
from jax.experimental import pallas as pl
from jax.experimental.pallas import tpu as pltpu
from jax.sharding import PartitionSpec as P

ALPHA = 0.5
OUTER_STEPS = 2
SWEEPS = 10
LOG2E = 1.4426950408889634

N = 2048
M = 1024
D = 256
NB = 512
MB = 256
F32 = jnp.float32
BF16 = jnp.bfloat16
LANES = 128

T_CHUNKS = 4
C1_CHUNKS = 2
TR = NB // T_CHUNKS
CR = NB // C1_CHUNKS
K_CHUNKS = 4
KR = 2 * NB // K_CHUNKS

S_T = 0
S_C2 = S_T + T_CHUNKS
S_Y = S_C2 + 1
S_P = S_Y + 1
S_X = S_P + 1
S_C1 = S_X + 1
ICI_SLOTS = S_C1 + C1_CHUNKS
F_T = S_P + 1
F_C2 = F_T + T_CHUNKS
F_Y = F_C2 + 1
F_P = F_Y + 1
S_C1P = F_P + 1
S_K1 = S_C1P + 1
S_K2 = S_K1 + K_CHUNKS
D2D_SLOTS = S_K2 + K_CHUNKS


def hint(value, multiple):
    return pl.multiple_of(value, multiple)


def sinkhorn(kern, plan_b, u_b, v_ref, q_ref):
    rb = 128
    blocks = N // rb
    cols = M // LANES

    def load(i, j):
        k = kern[pl.ds(hint(i * rb, rb), rb), j * LANES:(j + 1) * LANES]
        return k.reshape(rb // 8, 8, LANES)

    v_ref[...] = jnp.ones_like(v_ref)

    def sweep(_, carry):
        v = [v_ref[:, j * LANES:(j + 1) * LANES] for j in range(cols)]

        def row_sums(i):
            part = load(i, 0) * v[0][None]
            for j in range(1, cols):
                part = part + load(i, j) * v[j][None]
            return jnp.sum(part, axis=-1, keepdims=True)

        def accumulate(i, sums, acc):
            rows = pl.ds(hint(i * rb, rb), rb)
            u = plan_b[rows, :].reshape(rb // 8, 8, LANES) / sums
            u_b[rows, :] = u.reshape(rb, LANES)
            return tuple(acc[j] + jnp.sum(load(i, j) * u, axis=0) for j in range(cols))

        def body(i, state):
            sums, acc = state
            following = row_sums(i + 1)
            return following, accumulate(i, sums, acc)

        zero = tuple(jnp.zeros((8, LANES), F32) for _ in range(cols))
        sums, acc = lax.fori_loop(0, blocks - 1, body, (row_sums(0), zero))
        acc = accumulate(blocks - 1, sums, acc)
        for j in range(cols):
            col_sum = jnp.sum(acc[j], axis=0, keepdims=True)
            v_new = q_ref[:, j * LANES:(j + 1) * LANES] / col_sum
            v_ref[:, j * LANES:(j + 1) * LANES] = jnp.broadcast_to(v_new, (8, LANES))
        return carry

    lax.fori_loop(0, SWEEPS, sweep, 0)


def scaled_rows(kern, u_b, v_ref, row, count):
    parts = []
    u = u_b[pl.ds(row, count), :].reshape(count // 8, 8, LANES)
    for j in range(M // LANES):
        k = kern[pl.ds(row, count), j * LANES:(j + 1) * LANES].reshape(count // 8, 8, LANES)
        t = u * k * v_ref[:, j * LANES:(j + 1) * LANES][None]
        parts.append(t.reshape(count, LANES))
    return parts


def kernel(c1_hbm, c2_hbm, t0_hbm, p_hbm, q_ref, x_hbm, y_hbm, eps_ref, out_ref,
           c1_st, c2_st, t_st, x_st, y_st,
           t_all, c1_rows, c1_side, c2_all, y_all, x_rows, g_rows, a_buf,
           kern1, kern2, p_all, p_b, u_b, v_ref,
           load_sem, ici_send, ici_recv, d2d_send, d2d_recv):
    me = lax.axis_index("rows")
    chip = me // 2
    core = me % 2
    partner = chip * 2 + (1 - core)
    far = (1 - chip) * 2 + core
    far_partner = (1 - chip) * 2 + (1 - core)

    loads = [pltpu.make_async_copy(src, dst, load_sem.at[i]) for i, (src, dst) in enumerate((
        (t0_hbm, t_st), (c2_hbm, c2_st), (y_hbm, y_st), (p_hbm, p_all.at[me]), (x_hbm, x_st), (c1_hbm, c1_st)))]
    for copy in loads:
        copy.start()

    barrier = pltpu.get_barrier_semaphore()
    for peer in (partner, far):
        pl.semaphore_signal(barrier, inc=1, device_id={"rows": peer}, device_id_type=pl.DeviceIdType.MESH)
    pl.semaphore_wait(barrier, 2)

    def to_far(src, dst, slot):
        return pltpu.make_async_remote_copy(
            src_ref=src, dst_ref=dst, send_sem=ici_send.at[slot], recv_sem=ici_recv.at[slot],
            device_id={"rows": far}, device_id_type=pl.DeviceIdType.MESH)

    def to_partner(src, dst, slot):
        return pltpu.make_async_remote_copy(
            src_ref=src, dst_ref=dst, send_sem=d2d_send.at[slot], recv_sem=d2d_recv.at[slot],
            device_id={"rows": partner}, device_id_type=pl.DeviceIdType.MESH)

    def t_rows(owner, k):
        return t_all.at[pl.ds(hint(owner * NB + k * TR, TR), TR), :]

    def c2_diag(owner, owner_chip):
        return c2_all.at[pl.ds(hint(owner * MB, MB), MB), pl.ds(hint(owner_chip * 2 * MB, 2 * MB), 2 * MB)]

    def c2_full(owner):
        return c2_all.at[pl.ds(hint(owner * MB, MB), MB), :]

    def y_rows(owner):
        return y_all.at[pl.ds(hint(owner * MB, MB), MB), :]

    sends = []

    def go(copy):
        copy.start()
        sends.append(copy)

    loads[0].wait()
    for k in range(T_CHUNKS):
        t_all[pl.ds(hint(me * NB + k * TR, TR), TR), :] = t_st[k * TR:(k + 1) * TR, :].astype(BF16)
    for k in range(T_CHUNKS):
        go(to_far(t_rows(me, k), t_rows(me, k), S_T + k))
        go(to_partner(t_rows(me, k), t_rows(me, k), S_T + k))
    for copy in loads[1:5]:
        copy.wait()
    c2_all[pl.ds(hint(me * MB, MB), MB), :] = c2_st[...].astype(BF16)
    y_all[pl.ds(hint(me * MB, MB), MB), :] = y_st[...].astype(BF16)
    x_rows[:NB, :] = x_st[...].astype(BF16)
    loads[5].wait()
    c1_rows[:NB, :] = c1_st[...].astype(BF16)
    go(to_far(c2_diag(me, chip), c2_diag(me, chip), S_C2))
    go(to_far(y_rows(me), y_rows(me), S_Y))
    go(to_far(p_all.at[me], p_all.at[me], S_P))
    go(to_far(x_rows.at[:NB], x_rows.at[NB:], S_X))
    for k in range(C1_CHUNKS):
        cols = pl.ds(hint(chip * 2 * NB, 2 * NB), 2 * NB)
        go(to_far(c1_rows.at[k * CR:(k + 1) * CR, cols], c1_rows.at[NB + k * CR:NB + (k + 1) * CR, cols], S_C1 + k))
    go(to_partner(c2_full(me), c2_full(me), S_C2))
    go(to_partner(y_rows(me), y_rows(me), S_Y))
    go(to_partner(p_all.at[me], p_all.at[me], S_P))
    go(to_partner(c1_rows.at[:NB, pl.ds(hint(far_partner * NB, NB), NB)], c1_side, S_C1P))

    def mirror(src, src_row, src_col, dst, dst_row, dst_col, size):
        for i in range(size // LANES):
            for j in range(size // LANES):
                tile = src[pl.ds(hint(src_row + i * LANES, LANES), LANES), pl.ds(hint(src_col + j * LANES, LANES), LANES)]
                dst[pl.ds(hint(dst_row + j * LANES, LANES), LANES), pl.ds(hint(dst_col + i * LANES, LANES), LANES)] = (
                    tile.astype(F32).T.astype(BF16))

    mirror(c1_rows, 0, far * NB, c1_rows, NB, me * NB, NB)
    to_partner(c1_side, c1_side, S_C1P).wait_recv()
    mirror(c1_side, 0, 0, c1_rows, NB, partner * NB, NB)
    to_partner(c2_full(me), c2_full(partner), S_C2).wait_recv()
    mirror(c2_all, chip * 2 * MB, (1 - chip) * 2 * MB, c2_all, (1 - chip) * 2 * MB, chip * 2 * MB, 2 * MB)
    for k in range(T_CHUNKS):
        to_partner(t_rows(me, k), t_rows(partner, k), S_T + k).wait_recv()
    to_partner(y_rows(me), y_rows(partner), S_Y).wait_recv()
    to_partner(p_all.at[me], p_all.at[partner], S_P).wait_recv()

    for k in range(T_CHUNKS):
        to_far(t_rows(me, k), t_rows(far, k), S_T + k).wait_recv()
        go(to_partner(t_rows(far, k), t_rows(far, k), F_T + k))
    to_far(c2_diag(me, chip), c2_diag(far, 1 - chip), S_C2).wait_recv()
    go(to_partner(c2_diag(far, 1 - chip), c2_diag(far, 1 - chip), F_C2))
    to_far(y_rows(me), y_rows(far), S_Y).wait_recv()
    go(to_partner(y_rows(far), y_rows(far), F_Y))
    to_far(p_all.at[me], p_all.at[far], S_P).wait_recv()
    go(to_partner(p_all.at[far], p_all.at[far], F_P))
    to_far(x_rows.at[:NB], x_rows.at[NB:], S_X).wait_recv()
    for k in range(T_CHUNKS):
        to_partner(t_rows(far, k), t_rows(far_partner, k), F_T + k).wait_recv()
    to_partner(c2_diag(far, 1 - chip), c2_diag(far_partner, 1 - chip), F_C2).wait_recv()
    to_partner(y_rows(far), y_rows(far_partner), F_Y).wait_recv()
    to_partner(p_all.at[far], p_all.at[far_partner], F_P).wait_recv()

    for owner in range(4):
        for i in range(NB // LANES):
            block = jnp.broadcast_to(p_all[owner, i:i + 1, :], (LANES, LANES))
            p_b[owner * NB + i * LANES:owner * NB + (i + 1) * LANES, :] = block.T

    for h in range(2):
        for n in range(4):
            g = lax.dot_general(x_rows[h * NB:(h + 1) * NB, :], y_all[n * 256:(n + 1) * 256, :],
                                (((1,), (1,)), ((), ())), preferred_element_type=F32)
            g_rows[h * NB:(h + 1) * NB, n * 256:(n + 1) * 256] = (2.0 * ALPHA) * g

    scale = LOG2E / eps_ref[0, 0]

    def global_row(k):
        local = k * KR
        return jnp.where(local < NB, me * NB + local, far * NB + local - NB)

    def kernel_rows(kern, k):
        rows = pl.ds(hint(k * KR, KR), KR)
        for n in range(4):
            a_buf[:, n * 256:(n + 1) * 256] = jnp.dot(
                c1_rows[rows, :], t_all[:, n * 256:(n + 1) * 256], preferred_element_type=F32).astype(BF16)
        top = hint(global_row(k), KR)
        gain = []
        for n in range(4):
            b = jnp.dot(a_buf[...], c2_all[:, n * 256:(n + 1) * 256], preferred_element_type=F32)
            s = g_rows[rows, n * 256:(n + 1) * 256] + (2.0 * (1.0 - ALPHA)) * b
            kern[pl.ds(top, KR), n * 256:(n + 1) * 256] = s
            gain.append(jnp.max(s, axis=1, keepdims=True))
        peak = jnp.maximum(jnp.maximum(gain[0], gain[1]), jnp.maximum(gain[2], gain[3]))
        for n in range(4):
            s = kern[pl.ds(top, KR), n * 256:(n + 1) * 256]
            kern[pl.ds(top, KR), n * 256:(n + 1) * 256] = jnp.exp2((s - peak) * scale)

    def kern_slice(kern, base):
        return kern.at[pl.ds(hint(base, KR), KR), :]

    def share_rows(kern, k, slot):
        rows = kern_slice(kern, global_row(k))
        return to_partner(rows, rows, slot + k)

    def receive_rows(kern, k, slot):
        local = k * KR
        base = jnp.where(local < NB, partner * NB + local, far_partner * NB + local - NB)
        to_partner(kern_slice(kern, base), kern_slice(kern, base), slot + k).wait_recv()

    for step, (kern, slot) in enumerate(((kern1, S_K1), (kern2, S_K2))):
        def chunk(k, carry):
            kernel_rows(kern, k)
            share_rows(kern, k, slot).start()
            return carry
        if step == 0:
            lax.fori_loop(0, K_CHUNKS // 2, chunk, 0)
            for k in range(C1_CHUNKS):
                cols = pl.ds(hint((1 - chip) * 2 * NB, 2 * NB), 2 * NB)
                part = c1_rows.at[NB + k * CR:NB + (k + 1) * CR, cols]
                to_far(part, part, S_C1 + k).wait_recv()
            lax.fori_loop(K_CHUNKS // 2, K_CHUNKS, chunk, 0)
        else:
            lax.fori_loop(0, K_CHUNKS, chunk, 0)
        for k in range(K_CHUNKS):
            receive_rows(kern, k, slot)
        sinkhorn(kern, p_b, u_b, v_ref, q_ref)
        if step == 0:
            def next_plan(i, carry):
                row = hint(i * 64, 64)
                for j, t in enumerate(scaled_rows(kern, u_b, v_ref, row, 64)):
                    t_all[pl.ds(row, 64), j * LANES:(j + 1) * LANES] = t.astype(BF16)
                return carry
            for copy in sends:
                copy.wait_send()
            lax.fori_loop(0, N // 64, next_plan, 0)

    def result(i, carry):
        row = hint(i * 64, 64)
        for j, t in enumerate(scaled_rows(kern2, u_b, v_ref, hint(me * NB + row, 64), 64)):
            out_ref[pl.ds(row, 64), j * LANES:(j + 1) * LANES] = t
        return carry
    lax.fori_loop(0, NB // 64, result, 0)
    for kern, slot in ((kern1, S_K1), (kern2, S_K2)):
        for k in range(K_CHUNKS):
            share_rows(kern, k, slot).wait_send()


def solution(mesh):
    vmem = pl.BlockSpec(memory_space=pltpu.VMEM)
    hbm = pl.BlockSpec(memory_space=pl.ANY)
    smem = pl.BlockSpec(memory_space=pltpu.SMEM)

    def local_fgw(cost_src, cost_tgt, plan_init, mass_src, mass_tgt, feat_src, feat_tgt, epsilon):
        return pl.pallas_call(
            kernel,
            out_shape=jax.ShapeDtypeStruct((NB, M), F32),
            in_specs=[hbm, hbm, hbm, hbm, vmem, hbm, hbm, smem],
            out_specs=vmem,
            scratch_shapes=[
                pltpu.VMEM((NB, N), F32),
                pltpu.VMEM((MB, M), F32),
                pltpu.VMEM((NB, M), F32),
                pltpu.VMEM((NB, D), F32),
                pltpu.VMEM((MB, D), F32),
                pltpu.VMEM((N, M), BF16),
                pltpu.VMEM((2 * NB, N), BF16),
                pltpu.VMEM((NB, NB), BF16),
                pltpu.VMEM((M, M), BF16),
                pltpu.VMEM((M, D), BF16),
                pltpu.VMEM((2 * NB, D), BF16),
                pltpu.VMEM((2 * NB, M), F32),
                pltpu.VMEM((KR, M), BF16),
                pltpu.VMEM((N, M), F32),
                pltpu.VMEM((N, M), F32),
                pltpu.VMEM((4, NB // LANES, LANES), F32),
                pltpu.VMEM((N, LANES), F32),
                pltpu.VMEM((N, LANES), F32),
                pltpu.VMEM((8, M), F32),
                pltpu.SemaphoreType.DMA((6,)),
                pltpu.SemaphoreType.DMA((ICI_SLOTS,)),
                pltpu.SemaphoreType.DMA((ICI_SLOTS,)),
                pltpu.SemaphoreType.DMA((D2D_SLOTS,)),
                pltpu.SemaphoreType.DMA((D2D_SLOTS,)),
            ],
            compiler_params=pltpu.CompilerParams(
                collective_id=0, has_side_effects=True, vmem_limit_bytes=60000 * 1024),
        )(cost_src, cost_tgt, plan_init, mass_src.reshape(NB // LANES, LANES), mass_tgt.reshape(1, M),
          feat_src, feat_tgt, epsilon.reshape(1, 1))

    row_spec = P(('pairs', 'rows'), None)
    vec_spec = P(('pairs', 'rows'))
    in_specs = (row_spec, row_spec, row_spec, vec_spec, P('pairs'), row_spec, row_spec, P())
    return jax.shard_map(local_fgw, mesh=mesh, in_specs=in_specs, out_specs=row_spec, check_vma=False)
```

time: 267 us -> 145 us (0.54)
  Pallas kernels: 0 us -> 141 us
  blocking collectives: 137 us -> 0 us
  waiting for transfers between devices: 72.2 us -> 0 us
  other arithmetic: 23.3 us -> 0 us
  matrix products: 18.1 us -> 0 us
  between operations: 13.9 us -> 0.66 us
    pallas_call x0 -> x1, Pallas kernels: none -> 141 us  [local_fgw(): pl.pallas_call(kernel, out_shape=jax.ShapeDtypeStruct((NB, M), F32), in_s...]
    psum x20 -> x0, blocking collectives: 120 us -> none  [value_a14(): col_sum = lax.psum(jnp.sum(kernel * row_scale[:, None], axis=0), 'rows')]
    all_gather x3 -> x0, waiting for transfers between devices: 72.1 us -> none  [the longest x2 65.5 us: local_fgw(): lax.all_gather(transport.astype(jnp.bfloat16), 'rows', tiled=True)]
    dot_general x3 -> x0, matrix products: 18.1 us -> none  [the longest x2 17.7 us: local_fgw(): jnp.dot(prod_a.astype(jnp.bfloat16), tgt_all, preferred_element_type=jnp....]
    all_gather x1 -> x0, blocking collectives: 16.2 us -> none  [local_fgw(): feat_all = lax.all_gather(feat_tgt.astype(jnp.bfloat16), 'rows', tiled=True)]
    reduce_sum x40 -> x0, other arithmetic: 8.54 us -> none  [the longest x20 4.33 us: value_a14(): row_scale = mass_rows / jnp.sum(kernel * scales[1][None, :], axis=1)]
    convert_element_type x4 -> x0, other arithmetic: 6.84 us -> none  [the longest x2 4.53 us: local_fgw(): transport.astype(jnp.bfloat16)]
    exp x2 -> x0, other arithmetic: 4.02 us -> none  [gibbs_kernel(): jnp.exp(-(cost_rows - jnp.min(cost_rows, axis=1, keepdims=True)) / epsilon)]
  transfers between devices with their start and end apart: 3 -> 0, of which waited for: 3 -> 0; matrix products, arithmetic and copies ran while one was open for 1% -> 0% of each run, Pallas kernels for 0% -> 0%
where the time goes in v1:
time: 145 us
  Pallas kernels  141 us (97%)
  local copies, waits for them, and re-layouts  3.16 us (2%)
    pallas_call x1, Pallas kernels, local_fgw(): pl.pallas_call(kernel, out_shape=jax.ShapeDtypeStruct((NB, M), F32), in_s...  141 us
    unnamed x1, local copies, waits for them, and re-layouts  3.16 us

profile of v1, /device:TPU:0, one launch (start us, length us, event | category | flops | bytes accessed | tf_op | source)
XLA Modules:
  0.0 145.3 jit_solution(8876440408195049991)
XLA Ops:
  0.7 141.4 %shard_map.82 = f32[512,1024]{1,0:T(8,128)} custom-call(f32[512,2048]{1,0:T(8,128)} %c1_hbm.1, f32[256,1024]{1,0:T(8,128)} %c2_hbm.1, f32[512,1024]{1,0:T(8,128)} %t0_hbm.1, f32[4,128]{1,0:T(4,128)} %bitcast.5, f32[1,1024]{1,0:T(1,128)} %bitcast.4, f32[512,256]{1,0:T(8,128)} %x_hbm.1, f32[256,256]{1,0:T(8,128)} %y_hbm.1, f32[1,1]{1,0:T(1,128)} %bitcast.3.eps_ref), custom_call_target="tpu_custom_call" | custom-call | tf_op jit(solution)/shard_map/pallas_call | solution.py:301
  142.1 3.2 %copy.11 = f32[512,1024]{1,0:T(8,128)} copy(f32[512,1024]{1,0:T(8,128)} %shard_map.82) | data formatting | bytes 4194304
